TPU v7x, 32 devices: a whole 2x2x4 slice. The times are simulated.
32 devices in a mesh: group: 2 (over core), fsdp: 4 (over z), tp: 4 (over y, x).
Axes of the slice: x: 2, y: 2, z: 4, core: 2. Of those that a mesh axis runs over, the one named last changes fastest.
Arguments:
- text_embeds: bfloat16 [4096, 8192], P(('group', 'fsdp'), 'tp'), may hold values from -6 to 6
- image_embeds: bfloat16 [2048, 8192], P(('group', 'fsdp'), 'tp'), may hold values from -6 to 6
- key_weight: bfloat16 [8192, 512], P(('group', 'fsdp')), may hold values from -0.0625 to 0.0625
- key_bias: float32 [512], P('tp'), may hold values from -3 to 3
- key_cot: bfloat16 [4096, 512], P(('group', 'fsdp')), may hold values from -6 to 6
- image_owner: int32 [2048], P(('group', 'fsdp')), may hold values from 0 to 7, as said below
- image_slot: int32 [4096], P(('group', 'fsdp')), may hold values from -1 to 511, as said below
- seq_lengths: int32 [16], P(('group', 'fsdp')), may hold values from 248 to 256, as said below
Outputs:
- key_rows: bfloat16 [4096, 512], P(('group', 'fsdp'), 'tp')
- text_grad: bfloat16 [4096, 8192], P(('group', 'fsdp'), 'tp')
- image_grad: bfloat16 [2048, 8192], P(('group', 'fsdp'), 'tp')
- weight_grad: float32 [8192, 512], P(('group', 'fsdp'), 'tp')
Inputs may be any that keep to these rules, and one draw needn't show every extreme that they name: `image_owner`: A source block of 256 image tokens sends at most 64 of them to one owner, and some block sends exactly 64 to some owner; an owner takes at most 448 image tokens in all, and some owner takes exactly that many. Every image token has exactly one position, as step one says. `image_slot`: slots are distinct within an owner block, and image tokens sit only at live positions. `seq_lengths`: some sequence has length 256.
All inputs are finite; a program needn't handle non-finite values.
Results may differ from a plain program's by a relative error of at most 0.0046.
Values may be sent and summed in bfloat16 or wider, within the bound.
A program may use at most 64 MiB of HBM per device.

v0:
```python
import jax
import jax.numpy as jnp
from jax import lax
from jax.sharding import PartitionSpec as P

HEAD_DIM = 128
LENGTH = 256


ROPE_BASE = 1000000.0


def angles(row_total):
    position = (jnp.arange(row_total, dtype=jnp.int32) % LENGTH).astype(jnp.float32)
    frequency = ROPE_BASE ** (-(jnp.arange(HEAD_DIM // 2, dtype=jnp.float32) * 2.0) / HEAD_DIM)
    angle_table = position[:, None] * frequency[None, :]
    return (jnp.cos(angle_table), jnp.sin(angle_table))


def rotate(values, cosine, sine, direction):
    row_total = values.shape[0]
    by_head = values.reshape(row_total, -1, HEAD_DIM)
    half_dim = HEAD_DIM // 2
    front_half = by_head[..., :half_dim]
    second = by_head[..., half_dim:]
    cos_part = cosine[:, None, :]
    sin_part = direction * sine[:, None, :]
    rotated = jnp.concatenate(
        [front_half * cos_part - second * sin_part, second * cos_part + front_half * sin_part],
        axis=-1,
    )
    return rotated.reshape(row_total, -1)


def send_slots(owners, unit_count, capacity):
    onehot_marks = (owners[:, None] == jnp.arange(unit_count, dtype=jnp.int32)[None, :]).astype(
        jnp.int32
    )
    before = jnp.cumsum(onehot_marks, axis=0) - onehot_marks
    owner_rank = jnp.sum(before * onehot_marks, axis=1)
    return owners * capacity + owner_rank


def per_device(
    text_embeds, image_embeds, key_weight, key_bias, key_cot, image_owner, image_slot, seq_lengths
):
    row_count, columns = text_embeds.shape
    core_count = lax.axis_size("group")
    fsdp_count = lax.axis_size("fsdp")
    unit_count = core_count * fsdp_count
    capacity = row_count // unit_count
    head_cols = key_bias.shape[0]
    tp_index = lax.axis_index("tp")
    slots_out = send_slots(image_owner, unit_count, capacity)
    outgoing = (
        jnp.zeros((unit_count * capacity, columns), jnp.bfloat16).at[slots_out].set(image_embeds)
    )
    received = lax.all_to_all(
        outgoing.reshape(unit_count, capacity, columns),
        ("group", "fsdp"),
        split_axis=0,
        concat_axis=0,
        tiled=True,
    )
    received = received.reshape(unit_count * capacity, columns)
    is_image = image_slot >= 0
    hidden = jnp.where(is_image[:, None], received[jnp.maximum(image_slot, 0)], text_embeds)
    own_cols = lax.dynamic_slice_in_dim(key_weight, tp_index * head_cols, head_cols, 1)
    weight_cols = lax.all_gather(own_cols, ("group", "fsdp"), axis=0, tiled=True)
    weight_rows = lax.all_to_all(weight_cols, "tp", split_axis=0, concat_axis=1, tiled=True)
    position = jnp.arange(row_count, dtype=jnp.int32)
    seq_ids = position // LENGTH
    seq_marks = seq_ids[:, None] == jnp.arange(seq_lengths.shape[0], dtype=jnp.int32)[None, :]
    live_limit = jnp.sum(jnp.where(seq_marks, seq_lengths[None, :], 0), axis=1)
    live_mask = (position % LENGTH < live_limit).astype(jnp.float32)
    cosine, sine = angles(row_count)
    gathered = lax.all_gather(hidden, "tp", axis=1, tiled=True)
    projected = jnp.dot(gathered, weight_cols, preferred_element_type=jnp.float32) + key_bias
    key_rows = (rotate(projected, cosine, sine, 1.0) * live_mask[:, None]).astype(jnp.bfloat16)
    masked = key_cot.astype(jnp.float32) * live_mask[:, None]
    rotated_back = rotate(masked, cosine, sine, -1.0).astype(jnp.bfloat16)
    hidden_grad = lax.dot_general(
        rotated_back, weight_rows, (((1,), (1,)), ((), ())), preferred_element_type=jnp.float32
    ).astype(jnp.bfloat16)
    text_grad = jnp.where(is_image[:, None], jnp.zeros_like(hidden_grad), hidden_grad)
    returning = (
        jnp.zeros((unit_count * capacity, columns), jnp.bfloat16)
        .at[jnp.where(is_image, image_slot, unit_count * capacity)]
        .set(hidden_grad, mode="drop")
    )
    returned = lax.all_to_all(
        returning.reshape(unit_count, capacity, columns),
        ("group", "fsdp"),
        split_axis=0,
        concat_axis=0,
        tiled=True,
    )
    image_grad = returned.reshape(unit_count * capacity, columns)[slots_out]
    own_back = lax.dynamic_slice_in_dim(rotated_back, tp_index * head_cols, head_cols, 1)
    weight_grad = lax.psum_scatter(
        lax.dot_general(
            gathered, own_back, (((0,), (0,)), ((), ())), preferred_element_type=jnp.float32
        ),
        ("group", "fsdp"),
        scatter_dimension=0,
        tiled=True,
    )
    return (key_rows, text_grad, image_grad, weight_grad / row_count)


def solution(mesh):
    in_specs = (
        P(("group", "fsdp"), "tp"),
        P(("group", "fsdp"), "tp"),
        P(("group", "fsdp"), None),
        P("tp"),
        P(("group", "fsdp"), None),
        P(("group", "fsdp")),
        P(("group", "fsdp")),
        P(("group", "fsdp")),
    )
    out_specs = (
        P(("group", "fsdp"), "tp"),
        P(("group", "fsdp"), "tp"),
        P(("group", "fsdp"), "tp"),
        P(("group", "fsdp"), "tp"),
    )
    return jax.shard_map(
        per_device, mesh=mesh, in_specs=in_specs, out_specs=out_specs, check_vma=False
    )
```

profile of v0, /device:TPU:25, one launch (start us, length us, event | category | flops | bytes accessed | tf_op | source)
XLA Modules:
  0.0 357.2 jit_solution(3384726129702239781)
XLA Ops:
  10.2 4.4 %scatter_custom_fusion = bf16[512,2048]{1,0:T(8,128)(2,1)} fusion(s32[256]{0:T(256)S(1)} %compare_select_fusion.2, bf16[256,2048]{1,0:T(8,128)(2,1)} %param.9, bf16[]{:T(256)} %constant.53.clone.1), kind=kCustom, calls=%fused_computation.16 | custom fusion | bytes 2097664 | tf_op jit(solution)/shard_map/scatter | solution.py:56
  14.6 5.5 %all-to-all-start = ((bf16[8,64,2048]{2,1,0:T(8,128)(2,1)}), bf16[8,64,2048]{2,1,0:T(8,128)(2,1)S(1)}, u32[]{:S(2)}, u32[]{:S(2)}) async-start(bf16[8,64,2048]{2,1,0:T(8,128)(2,1)} %bitcast.37), calls=%async_computation | async-start | bytes 4194304 | tf_op jit(solution)/shard_map/all_to_all | solution.py:58
  20.9 2.0 copy.18
  23.1 2.2 convert_multiply_fusion
  25.2 47.0 %all-to-all-done = bf16[8,64,2048]{2,1,0:T(8,128)(2,1)S(1)} async-done(((bf16[8,64,2048]{2,1,0:T(8,128)(2,1)}), bf16[8,64,2048]{2,1,0:T(8,128)(2,1)S(1)}, u32[]{:S(2)}, u32[]{:S(2)}) %all-to-all-start) | async-done | bytes 2097184 | tf_op jit(solution)/shard_map/all_to_all | solution.py:58
  72.6 4.4 %all-to-all-start.1 = ((bf16[4,2048,128]{2,1,0:T(8,128)(2,1)}), bf16[4,2048,128]{2,1,0:T(8,128)(2,1)}, u32[]{:S(2)}, u32[]{:S(2)}) async-start(bf16[4,2048,128]{2,1,0:T(8,128)(2,1)} %bitcast.39), calls=%async_computation.1 | async-start | bytes 4194304 | tf_op jit(solution)/shard_map/all_to_all | solution.py:70
  77.2 2.2 fusion.30
  79.4 2.4 copy.24
  81.8 2.4 copy.23
  84.2 1.0 multiply_cosine_fusion
  85.2 1.9 multiply_subtract_fusion
  87.0 1.1 maximum_convert_fusion
  88.1 3.3 gather_fusion
  91.4 10.5 %all-to-all-done.1 = bf16[4,2048,128]{2,1,0:T(8,128)(2,1)} async-done(((bf16[4,2048,128]{2,1,0:T(8,128)(2,1)}), bf16[4,2048,128]{2,1,0:T(8,128)(2,1)}, u32[]{:S(2)}, u32[]{:S(2)}) %all-to-all-start.1) | async-done | bytes 2097184 | tf_op jit(solution)/shard_map/all_to_all | solution.py:70
  101.9 7.2 %broadcast_select_fusion = (bf16[512,2048]{1,0:T(8,128)(2,1)}, bf16[512,2048]{1,0:T(8,128)(2,1)}, bf16[512,2048]{1,0:T(8,128)(2,1)}) fusion(pred[512]{0:T(512)(128)(4,1)S(1)} %broadcast_compare_fusion, bf16[512,2048]{1,0:T(8,128)(2,1)} %gather_fusion, bf16[512,2048]{1,0:T(8,128)(2,1)} %param.8, bf16[512,4,128]{2,0,1:T(8,128)(2,1)} %maximum_convert_fusion, ...), kind=kOutput, calls=%fused_computation.6 | convolution fusion | flops 1076887552 | bytes 13107712 | tf_op jit(solution)/shard_map/dot_general | solution.py:82
  110.3 96.7 %all-gather.3.cloned.1.call-done = bf16[512,8192]{1,0:T(8,128)(2,1)} async-done(((bf16[512,2048]{1,0:T(8,128)(2,1)}), bf16[512,8192]{1,0:T(8,128)(2,1)}) %all-gather.3.cloned.1.call-update) | async-done | bytes 8388624 | tf_op jit(solution)/shard_map/all_gather | solution.py:77
  207.0 7.7 %fusion.15 = f32[8192,128]{1,0:T(8,128)} fusion(bf16[512,8192]{1,0:T(8,128)(2,1)} %all-gather.3.cloned.1.call-done, bf16[512,512]{0,1:T(8,128)(2,1)S(1)} %bitcast.41, s32[]{:T(128)S(6)} %select_n.70), kind=kOutput, calls=%fused_computation.33 | convolution fusion | flops 1073741824 | bytes 12713988 | tf_op jit(solution)/shard_map/dot_general | solution.py:101
  214.7 6.1 %scatter_custom_fusion.1 = bf16[512,2048]{1,0:T(8,128)(2,1)} fusion(s32[512]{0:T(512)S(1)} %get-tuple-element.24, bf16[512,2048]{1,0:T(8,128)(2,1)} %get-tuple-element.28, bf16[]{:T(256)} %constant.53.clone.1), kind=kCustom, calls=%fused_computation.14 | custom fusion | bytes 2097664 | tf_op jit(solution)/shard_map/scatter | solution.py:89
  220.8 5.5 %all-to-all-start.2 = ((bf16[8,64,2048]{2,1,0:T(8,128)(2,1)}), bf16[8,64,2048]{2,1,0:T(8,128)(2,1)S(1)}, u32[]{:S(2)}, u32[]{:S(2)}) async-start(bf16[8,64,2048]{2,1,0:T(8,128)(2,1)} %bitcast.38), calls=%async_computation.2 | async-start | bytes 4194304 | tf_op jit(solution)/shard_map/all_to_all | solution.py:91
  226.4 67.3 %all-to-all-done.2 = bf16[8,64,2048]{2,1,0:T(8,128)(2,1)S(1)} async-done(((bf16[8,64,2048]{2,1,0:T(8,128)(2,1)}), bf16[8,64,2048]{2,1,0:T(8,128)(2,1)S(1)}, u32[]{:S(2)}, u32[]{:S(2)}) %all-to-all-start.2) | async-done | bytes 2097184 | tf_op jit(solution)/shard_map/all_to_all | solution.py:91
  293.7 2.3 gather_fusion.1
  296.1 6.9 %fusion.1 = f32[512,1,128]{0,2,1:T(8,128)S(1)} fusion(bf16[512,8192]{1,0:T(8,128)(2,1)} %all-gather.3.cloned.1.call-done, bf16[8192,128]{1,0:T(8,128)(2,1)} %all-gather.5.cloned.1.call-done, f32[128]{0:T(128)S(1)} %copy-done.3), kind=kOutput, calls=%fused_computation.9 | convolution fusion | flops 1073807360 | bytes 10748416 | tf_op jit(solution)/shard_map/dot_general | solution.py:78
  304.3 44.4 %reduce-scatter.2.cloned.1.call-done = f32[1024,128]{1,0:T(8,128)} async-done(((f32[8192,128]{1,0:T(8,128)}), f32[1024,128]{1,0:T(8,128)}) %reduce-scatter.2.cloned.1.call-update) | async-done | bytes 524304 | tf_op jit(solution)/shard_map/reduce_scatter | solution.py:100
  348.8 1.9 broadcast_multiply_fusion
  (38 shorter events, 7.0 us)
Async XLA Ops:
  7.2 13.0 %copy-start = (bf16[1024,512]{1,0:T(8,128)(2,1)S(1)}, bf16[1024,512]{1,0:T(8,128)(2,1)}, u32[]{:S(2)}) copy-start(bf16[1024,512]{1,0:T(8,128)(2,1)} %param.10) | copy-start | bytes 3145732
  14.6 8.3 %copy-start.4 = (s32[2]{0:T(128)S(1)}, s32[2]{0:T(128)}, u32[]{:S(2)}) copy-start(s32[2]{0:T(128)} %param.15) | copy-start | bytes 28
  14.6 57.6 %all-to-all-start = ((bf16[8,64,2048]{2,1,0:T(8,128)(2,1)}), bf16[8,64,2048]{2,1,0:T(8,128)(2,1)S(1)}, u32[]{:S(2)}, u32[]{:S(2)}) async-start(bf16[8,64,2048]{2,1,0:T(8,128)(2,1)} %bitcast.37), calls=%async_computation | async-start | bytes 4194304 | tf_op jit(solution)/shard_map/all_to_all | solution.py:58
  20.1 52.5 %all-gather.5.cloned.1.call-start = ((), (), s32[]{:S(2)}) async-start(), calls=%async_computation.5 | async-start | bytes 2359296 | tf_op jit(solution)/shard_map/all_gather | solution.py:69
  72.6 29.2 %all-to-all-start.1 = ((bf16[4,2048,128]{2,1,0:T(8,128)(2,1)}), bf16[4,2048,128]{2,1,0:T(8,128)(2,1)}, u32[]{:S(2)}, u32[]{:S(2)}) async-start(bf16[4,2048,128]{2,1,0:T(8,128)(2,1)} %bitcast.39), calls=%async_computation.1 | async-start | bytes 4194304 | tf_op jit(solution)/shard_map/all_to_all | solution.py:70
  77.1 129.9 %all-gather.3.cloned.1.call-start = ((), (), s32[]{:S(2)}) async-start(), calls=%async_computation.4 | async-start | bytes 10485760 | tf_op jit(solution)/shard_map/all_gather | solution.py:77
  79.4 4.7 %copy-start.2 = (s32[512]{0:T(512)S(1)}, s32[512]{0:T(512)}, u32[]{:S(2)}) copy-start(s32[512]{0:T(512)} %param.14) | copy-start | bytes 6148
  109.0 1.0 copy-start.1
  109.1 239.7 %reduce-scatter.2.cloned.1.call-start = ((), (), s32[]{:S(2)}) async-start(), calls=%async_computation.6 | async-start | bytes 4718592 | tf_op jit(solution)/shard_map/reduce_scatter | solution.py:100
  220.8 72.9 %all-to-all-start.2 = ((bf16[8,64,2048]{2,1,0:T(8,128)(2,1)}), bf16[8,64,2048]{2,1,0:T(8,128)(2,1)S(1)}, u32[]{:S(2)}, u32[]{:S(2)}) async-start(bf16[8,64,2048]{2,1,0:T(8,128)(2,1)} %bitcast.38), calls=%async_computation.2 | async-start | bytes 4194304 | tf_op jit(solution)/shard_map/all_to_all | solution.py:91
  293.7 2.3 copy-start.3
Sparse Core Ops, SparseCore 0:
  22.5 50.0 all-gather.4
  109.2 97.7 all-gather.2
  214.8 133.9 reduce-scatter.1
where the time goes:
time: 359 us; the launch traced here: 357 us
  waiting for transfers between devices  266 us (74%)
  local copies, waits for them, and re-layouts  27.9 us (8%)
  matrix products  21.8 us (6%)
  starting transfers between devices  15.8 us (4%)
  between operations  13.8 us (4%)
  other arithmetic  11.5 us (3%)
    all_gather x1, waiting for transfers between devices, per_device(): gathered = lax.all_gather(hidden, 'tp', axis=1, tiled=True)  96.7 us
    all_to_all x1, waiting for transfers between devices, per_device(): lax.all_to_all(returning.reshape(unit_count, capacity, columns), ('group'...  67.3 us
    all_to_all x1, waiting for transfers between devices, per_device(): lax.all_to_all(outgoing.reshape(unit_count, capacity, columns), ('group',...  47 us
    reduce_scatter x1, waiting for transfers between devices, per_device(): lax.psum_scatter(lax.dot_general(gathered, own_back, (((0,), (0,)), ((),...  44.4 us
    all_to_all x1, waiting for transfers between devices, per_device(): lax.all_to_all(weight_cols, 'tp', split_axis=0, concat_axis=1, tiled=True)  10.5 us
    unnamed x14, local copies, waits for them, and re-layouts  8.33 us
    dot_general x1, matrix products, per_device(): lax.dot_general(gathered, own_back, (((0,), (0,)), ((), ())), preferred_e...  7.7 us
    dot_general x1, matrix products, per_device(): lax.dot_general(rotated_back, weight_rows, (((1,), (1,)), ((), ())), pref...  7.18 us
  transfers between devices with their start and end apart: 6, of which 6 were waited for; matrix products, arithmetic and copies ran while one was open for 10% of the time, Pallas kernels for 0%

commit v1 on v0

v1 whole, which is shorter than its diff:
```python
import jax
import jax.numpy as jnp
from jax import lax
from jax.sharding import PartitionSpec as P

HEAD_DIM = 128
LENGTH = 256


ROPE_BASE = 1000000.0


def angles(row_total):
    position = (jnp.arange(row_total, dtype=jnp.int32) % LENGTH).astype(jnp.float32)
    frequency = ROPE_BASE ** (-(jnp.arange(HEAD_DIM // 2, dtype=jnp.float32) * 2.0) / HEAD_DIM)
    angle_table = position[:, None] * frequency[None, :]
    return (jnp.cos(angle_table), jnp.sin(angle_table))


def rotate(values, cosine, sine, direction):
    row_total = values.shape[0]
    by_head = values.reshape(row_total, -1, HEAD_DIM)
    half_dim = HEAD_DIM // 2
    front_half = by_head[..., :half_dim]
    second = by_head[..., half_dim:]
    cos_part = cosine[:, None, :]
    sin_part = direction * sine[:, None, :]
    rotated = jnp.concatenate(
        [front_half * cos_part - second * sin_part, second * cos_part + front_half * sin_part],
        axis=-1,
    )
    return rotated.reshape(row_total, -1)


def send_slots(owners, unit_count, capacity):
    onehot_marks = (owners[:, None] == jnp.arange(unit_count, dtype=jnp.int32)[None, :]).astype(
        jnp.int32
    )
    before = jnp.cumsum(onehot_marks, axis=0) - onehot_marks
    owner_rank = jnp.sum(before * onehot_marks, axis=1)
    return owners * capacity + owner_rank


def per_device(
    text_embeds, image_embeds, key_weight, key_bias, key_cot, image_owner, image_slot, seq_lengths
):
    row_count, columns = text_embeds.shape
    image_count = image_embeds.shape[0]
    units = ("group", "fsdp")
    core_count = lax.axis_size("group")
    fsdp_count = lax.axis_size("fsdp")
    tp_count = lax.axis_size("tp")
    unit_count = core_count * fsdp_count
    capacity = row_count // unit_count
    slot_count = unit_count * capacity
    head_cols = key_bias.shape[0]
    key_cols = head_cols * tp_count
    weight_block = key_weight.shape[0]
    halves = unit_count // tp_count
    tp_index = lax.axis_index("tp")

    position = jnp.arange(row_count, dtype=jnp.int32)
    seq_ids = position // LENGTH
    seq_marks = seq_ids[:, None] == jnp.arange(seq_lengths.shape[0], dtype=jnp.int32)[None, :]
    live_limit = jnp.sum(jnp.where(seq_marks, seq_lengths[None, :], 0), axis=1)
    live_mask = (position % LENGTH < live_limit).astype(jnp.float32)
    cosine, sine = angles(row_count)
    masked = key_cot.astype(jnp.float32) * live_mask[:, None]
    rotated_back = rotate(masked, cosine, sine, -1.0).astype(jnp.bfloat16)
    is_image = image_slot >= 0
    text_back = jnp.where(is_image[:, None], jnp.zeros_like(rotated_back), rotated_back)

    slot_ids = jnp.arange(slot_count, dtype=jnp.int32)
    place = (image_slot[:, None] == slot_ids[None, :]).astype(jnp.bfloat16)
    returning = lax.dot_general(
        place, rotated_back, (((0,), (0,)), ((), ())), preferred_element_type=jnp.float32
    ).astype(jnp.bfloat16)
    returned = lax.all_to_all(
        returning.reshape(unit_count, capacity, key_cols), units, split_axis=0, concat_axis=0,
        tiled=True,
    ).reshape(slot_count, key_cols)
    slots_out = send_slots(image_owner, unit_count, capacity)
    pick = (slots_out[:, None] == slot_ids[None, :]).astype(jnp.bfloat16)
    image_back = jnp.dot(pick, returned, preferred_element_type=jnp.float32).astype(jnp.bfloat16)

    piece_rows = weight_block // tp_count
    own_piece = lax.dynamic_slice_in_dim(key_weight, tp_index * piece_rows, piece_rows, 0)
    moves = []
    for unit in range(unit_count):
        for part in range(tp_count):
            target = (unit % halves) * tp_count + part
            moves.append((unit * tp_count + part, target * tp_count + unit // halves))
    own_piece = lax.ppermute(own_piece, units + ("tp",), moves)
    weight_rows = lax.all_gather(own_piece, units, axis=0, tiled=True)

    weight_part = lax.dot_general(
        text_embeds, text_back, (((0,), (0,)), ((), ())), preferred_element_type=jnp.float32
    )
    weight_part = (
        weight_part
        + lax.dot_general(
            image_embeds, image_back, (((0,), (0,)), ((), ())), preferred_element_type=jnp.float32
        )
    ).astype(jnp.bfloat16)
    weight_part = weight_part.reshape(halves, weight_block, tp_count, head_cols)
    weight_part = weight_part.transpose(0, 2, 1, 3).reshape(unit_count, weight_block, head_cols)
    shares = lax.all_to_all(weight_part, units, split_axis=0, concat_axis=0, tiled=True)
    weight_grad = jnp.sum(shares.astype(jnp.float32), axis=0) / row_count
    weight_grad = lax.ppermute(weight_grad, units + ("tp",), [(b, a) for a, b in moves])

    text_part = jnp.dot(text_embeds, weight_rows, preferred_element_type=jnp.float32)
    image_part = jnp.dot(image_embeds, weight_rows, preferred_element_type=jnp.float32)
    both = jnp.concatenate(
        [text_part.astype(jnp.bfloat16), image_part.astype(jnp.bfloat16)], axis=0
    )
    both = both.reshape(row_count + image_count, tp_count, head_cols).transpose(1, 0, 2)
    both = lax.all_to_all(both, "tp", split_axis=0, concat_axis=0, tiled=True)
    both = jnp.sum(both.astype(jnp.float32), axis=0)
    image_proj = both[row_count:].astype(jnp.bfloat16)
    outgoing = lax.dot_general(
        pick, image_proj, (((0,), (0,)), ((), ())), preferred_element_type=jnp.float32
    ).astype(jnp.bfloat16)
    received = lax.all_to_all(
        outgoing.reshape(unit_count, capacity, head_cols), units, split_axis=0, concat_axis=0,
        tiled=True,
    ).reshape(slot_count, head_cols)
    placed = jnp.dot(place, received, preferred_element_type=jnp.float32)
    projected = jnp.where(is_image[:, None], placed, both[:row_count]) + key_bias
    key_rows = (rotate(projected, cosine, sine, 1.0) * live_mask[:, None]).astype(jnp.bfloat16)

    contract = (((1,), (1,)), ((), ()))
    text_grad = lax.dot_general(
        text_back, weight_rows, contract, preferred_element_type=jnp.float32
    ).astype(jnp.bfloat16)
    image_grad = lax.dot_general(
        image_back, weight_rows, contract, preferred_element_type=jnp.float32
    ).astype(jnp.bfloat16)
    return (key_rows, text_grad, image_grad, weight_grad)


def solution(mesh):
    in_specs = (
        P(("group", "fsdp"), "tp"),
        P(("group", "fsdp"), "tp"),
        P(("group", "fsdp"), None),
        P("tp"),
        P(("group", "fsdp"), None),
        P(("group", "fsdp")),
        P(("group", "fsdp")),
        P(("group", "fsdp")),
    )
    out_specs = (
        P(("group", "fsdp"), "tp"),
        P(("group", "fsdp"), "tp"),
        P(("group", "fsdp"), "tp"),
        P(("group", "fsdp"), "tp"),
    )
    return jax.shard_map(
        per_device, mesh=mesh, in_specs=in_specs, out_specs=out_specs, check_vma=False
    )
```

time: 359 us -> 194 us (0.54)
  the two profiles are of different devices: /device:TPU:25 before, /device:TPU:4 now
where the time goes in v1:
time: 194 us; the launch traced here: 193 us
  waiting for transfers between devices  102 us (53%)
  starting transfers between devices  30.6 us (16%)
  matrix products  20 us (10%)
  local copies, waits for them, and re-layouts  16 us (8%)
  between operations  14.3 us (7%)
  other arithmetic  9.87 us (5%)
    all_to_all x1, waiting for transfers between devices, per_device(): lax.all_to_all(weight_part, units, split_axis=0, concat_axis=0, tiled=True)  40.3 us
    all_to_all x1, waiting for transfers between devices, per_device(): lax.all_to_all(returning.reshape(unit_count, capacity, key_cols), units,...  27.9 us
    ppermute x1, waiting for transfers between devices, per_device(): lax.ppermute(weight_grad, units + ('tp',), [(b, a) for a, b in moves])  22.2 us
    all_to_all x1, starting transfers between devices, per_device(): lax.all_to_all(returning.reshape(unit_count, capacity, key_cols), units,...  12.3 us
    reshape x2, local copies, waits for them, and re-layouts, per_device(): weight_part = weight_part.reshape(halves, weight_block, tp_count, head_cols)  10.6 us
    ppermute x1, waiting for transfers between devices, per_device(): own_piece = lax.ppermute(own_piece, units + ('tp',), moves)  6.21 us
    ppermute x1, starting transfers between devices, per_device(): own_piece = lax.ppermute(own_piece, units + ('tp',), moves)  4.44 us
    all_to_all x1, starting transfers between devices, per_device(): lax.all_to_all(weight_part, units, split_axis=0, concat_axis=0, tiled=True)  4.34 us
  transfers between devices with their start and end apart: 7, of which 6 were waited for; matrix products, arithmetic and copies ran while one was open for 20% of the time, Pallas kernels for 0%

profile of v1, /device:TPU:4, one launch (start us, length us, event | category | flops | bytes accessed | tf_op | source)
XLA Modules:
  0.0 192.9 jit_solution(3244209896760307135)
XLA Ops:
  8.3 4.4 %collective-permute-start = (bf16[256,512]{1,0:T(8,128)(2,1)S(1)}, bf16[256,512]{1,0:T(8,128)(2,1)S(1)}, u32[]{:S(2)}, u32[]{:S(2)}) collective-permute-start(bf16[256,512]{1,0:T(8,128)(2,1)S(1)} %constant_dynamic-slice_fusion), channel_id=1, source_target_pairs={{0,0},{1,4},{2,8},{3,12},{4,16},{5,20},{6,24},{7,28},{8,1},{9,5},{... | collective-permute-start | bytes 786440 | tf_op jit(solution)/shard_map/ppermute | solution.py:93
  12.8 6.2 %collective-permute-done = bf16[256,512]{1,0:T(8,128)(2,1)S(1)} collective-permute-done((bf16[256,512]{1,0:T(8,128)(2,1)S(1)}, bf16[256,512]{1,0:T(8,128)(2,1)S(1)}, u32[]{:S(2)}, u32[]{:S(2)}) %collective-permute-start) | collective-permute-done | bytes 262176 | tf_op jit(solution)/shard_map/ppermute | solution.py:93
  20.5 2.1 %convert_multiply_fusion = f32[512,512]{1,0:T(8,128)} fusion(bf16[512,512]{1,0:T(8,128)(2,1)} %param.12, f32[512]{0:T(512)S(1)} %fusion.31), kind=kLoop, calls=%fused_computation.18 | loop fusion | flops 524288 | bytes 1574912 | tf_op jit(solution)/shard_map/mul | solution.py:68
  22.6 1.6 reshape.214
  26.8 1.4 convolution_convert_fusion.3
  28.2 12.3 %all-to-all-start.2 = ((bf16[8,64,512]{2,1,0:T(8,128)(2,1)}), bf16[8,64,512]{2,1,0:T(8,128)(2,1)S(1)}, u32[]{:S(2)}, u32[]{:S(2)}) async-start(bf16[8,64,512]{2,1,0:T(8,128)(2,1)} %bitcast.63), calls=%async_computation.2 | async-start | bytes 1048576 | tf_op jit(solution)/shard_map/all_to_all | solution.py:78
  41.4 27.9 %all-to-all-done.2 = bf16[8,64,512]{2,1,0:T(8,128)(2,1)S(1)} async-done(((bf16[8,64,512]{2,1,0:T(8,128)(2,1)}), bf16[8,64,512]{2,1,0:T(8,128)(2,1)S(1)}, u32[]{:S(2)}, u32[]{:S(2)}) %all-to-all-start.2) | async-done | bytes 524320 | tf_op jit(solution)/shard_map/all_to_all | solution.py:78
  70.4 2.6 %all-gather.2.cloned.1.call-done = bf16[2048,512]{1,0:T(8,128)(2,1)} async-done(((bf16[256,512]{1,0:T(8,128)(2,1)}), bf16[2048,512]{1,0:T(8,128)(2,1)}) %all-gather.2.cloned.1.call-update) | async-done | bytes 2097168 | tf_op jit(solution)/shard_map/all_gather | solution.py:94
  73.0 3.0 %fusion.1 = bf16[512,512]{1,0:T(8,128)(2,1)S(1)} fusion(bf16[512,2048]{1,0:T(8,128)(2,1)S(1)} %copy-done, bf16[2048,512]{1,0:T(8,128)(2,1)} %all-gather.2.cloned.1.call-done), kind=kOutput, calls=%fused_computation.8 | convolution fusion | flops 1074003968 | bytes 4718592 | tf_op jit(solution)/shard_map/dot_general | solution.py:111
  77.8 4.2 %all-to-all-start = ((bf16[4,768,128]{2,1,0:T(8,128)(2,1)}), bf16[4,768,128]{2,1,0:T(8,128)(2,1)S(1)}, u32[]{:S(2)}, u32[]{:S(2)}) async-start(bf16[4,768,128]{2,1,0:T(8,128)(2,1)} %bitcast_bitcast_fusion), calls=%async_computation | async-start | bytes 1572864 | tf_op jit(solution)/shard_map/all_to_all | solution.py:117
  82.0 2.0 %fusion.34 = f32[512,2048]{1,0:T(8,128)S(1)} fusion(bf16[256,512]{1,0:T(8,128)(2,1)} %convolution_convert_fusion.5, bf16[256,2048]{1,0:T(8,128)(2,1)} %param.9), kind=kOutput, calls=%fused_computation.75 | convolution fusion | flops 536870912 | bytes 5505024 | tf_op jit(solution)/shard_map/dot_general | solution.py:101
  84.0 2.8 %fusion = bf16[2048,512]{0,1:T(8,128)(2,1)} fusion(f32[512,2048]{1,0:T(8,128)S(1)} %fusion.34, bf16[512,2048]{1,0:T(8,128)(2,1)S(1)} %copy-done, pred[512]{0:T(512)(128)(4,1)S(1)} %broadcast_compare_fusion, bf16[64,8,4,128]{3,2,1,0:T(4,128)(2,1)S(1)} %bitcast.60), kind=kOutput, calls=%fused_computation.3 | convolution fusion | flops 1076101120 | bytes 8913408 | tf_op jit(solution)/shard_map/dot_general | solution.py:96
  86.8 4.5 %reshape.217 = bf16[2,1024,4,128]{1,0,3,2:T(2,128)(2,1)} reshape(bf16[2048,512]{0,1:T(8,128)(2,1)} %fusion) | data formatting | bytes 4194304 | tf_op jit(solution)/shard_map/reshape | solution.py:105
  91.3 6.2 %copy.23 = bf16[2,1024,4,128]{3,1,2,0:T(8,128)(2,1)} copy(bf16[2,1024,4,128]{1,0,3,2:T(2,128)(2,1)} %reshape.217) | data formatting | bytes 4194304 | tf_op jit(solution)/shard_map/reshape | solution.py:105
  97.4 4.3 %all-to-all-start.3 = ((bf16[8,1024,128]{2,1,0:T(8,128)(2,1)}), bf16[8,1024,128]{2,1,0:T(8,128)(2,1)}, u32[]{:S(2)}, u32[]{:S(2)}) async-start(bf16[8,1024,128]{2,1,0:T(8,128)(2,1)} %bitcast.58), calls=%async_computation.3 | async-start | bytes 4194304 | tf_op jit(solution)/shard_map/all_to_all | solution.py:107
  101.8 3.5 %convolution_convert_fusion.1 = bf16[256,2048]{1,0:T(8,128)(2,1)} fusion(bf16[256,512]{1,0:T(8,128)(2,1)} %convolution_convert_fusion.5, bf16[2048,512]{1,0:T(8,128)(2,1)} %all-gather.2.cloned.1.call-done), kind=kOutput, calls=%fused_computation.4 | convolution fusion | flops 537395200 | bytes 3407872 | tf_op jit(solution)/shard_map/dot_general | solution.py:135
  105.3 2.6 %convolution_convert_fusion = bf16[512,2048]{1,0:T(8,128)(2,1)} fusion(bf16[2048,512]{1,0:T(8,128)(2,1)S(1)} %copy-done.2, pred[512]{0:T(512)(128)(4,1)S(1)} %broadcast_compare_fusion, bf16[64,8,4,128]{3,2,1,0:T(4,128)(2,1)S(1)} %bitcast.61), kind=kOutput, calls=%fused_computation.2 | convolution fusion | flops 1075052544 | bytes 4719104 | tf_op jit(solution)/shard_map/dot_general | solution.py:132
  108.2 1.7 convolution_convert_fusion.6
  110.0 40.3 %all-to-all-done.3 = bf16[8,1024,128]{2,1,0:T(8,128)(2,1)} async-done(((bf16[8,1024,128]{2,1,0:T(8,128)(2,1)}), bf16[8,1024,128]{2,1,0:T(8,128)(2,1)}, u32[]{:S(2)}, u32[]{:S(2)}) %all-to-all-start.3) | async-done | bytes 2097184 | tf_op jit(solution)/shard_map/all_to_all | solution.py:107
  150.3 3.4 %all-to-all-start.1 = ((bf16[8,64,128]{2,1,0:T(8,128)(2,1)}), bf16[8,64,128]{2,1,0:T(8,128)(2,1)S(1)}, u32[]{:S(2)}, u32[]{:S(2)}) async-start(bf16[8,64,128]{2,1,0:T(8,128)(2,1)} %bitcast.6), calls=%async_computation.1 | async-start | bytes 262144 | tf_op jit(solution)/shard_map/all_to_all | solution.py:123
  153.7 1.9 convert_reduce_fusion
  155.6 1.9 %collective-permute-start.1 = (f32[1024,128]{1,0:T(8,128)S(1)}, f32[1024,128]{1,0:T(8,128)S(1)}, u32[]{:S(2)}, u32[]{:S(2)}) collective-permute-start(f32[1024,128]{1,0:T(8,128)S(1)} %broadcast_multiply_fusion), channel_id=1, source_target_pairs={{0,0},{4,1},{8,2},{12,3},{16,4},{20,5},{24,6},{28,7},{1,8},{5,9},{... | collective-permute-start | bytes 1572872 | tf_op jit(solution)/shard_map/ppermute | solution.py:109
  157.6 2.9 %all-to-all-done.1 = bf16[8,64,128]{2,1,0:T(8,128)(2,1)S(1)} async-done(((bf16[8,64,128]{2,1,0:T(8,128)(2,1)}), bf16[8,64,128]{2,1,0:T(8,128)(2,1)S(1)}, u32[]{:S(2)}, u32[]{:S(2)}) %all-to-all-start.1) | async-done | bytes 131104 | tf_op jit(solution)/shard_map/all_to_all | solution.py:123
  163.0 22.2 %collective-permute-done.1 = f32[1024,128]{1,0:T(8,128)S(1)} collective-permute-done((f32[1024,128]{1,0:T(8,128)S(1)}, f32[1024,128]{1,0:T(8,128)S(1)}, u32[]{:S(2)}, u32[]{:S(2)}) %collective-permute-start.1) | collective-permute-done | bytes 524320 | tf_op jit(solution)/shard_map/ppermute | solution.py:109
  (48 shorter events, 12.5 us)
Async XLA Ops:
  7.2 65.8 %copy-start = (bf16[512,2048]{1,0:T(8,128)(2,1)S(1)}, bf16[512,2048]{1,0:T(8,128)(2,1)}, u32[]{:S(2)}) copy-start(bf16[512,2048]{1,0:T(8,128)(2,1)} %param.8) | copy-start | bytes 6291460
  7.2 65.8 %all-gather.2.cloned.1.call-start = ((), (), s32[]{:S(2)}) async-start(), calls=%async_computation.4 | async-start | bytes 2359296 | tf_op jit(solution)/shard_map/all_gather | solution.py:94
  8.3 10.7 %collective-permute-start = (bf16[256,512]{1,0:T(8,128)(2,1)S(1)}, bf16[256,512]{1,0:T(8,128)(2,1)S(1)}, u32[]{:S(2)}, u32[]{:S(2)}) collective-permute-start(bf16[256,512]{1,0:T(8,128)(2,1)S(1)} %constant_dynamic-slice_fusion), channel_id=1, source_target_pairs={{0,0},{1,4},{2,8},{3,12},{4,16},{5,20},{6,24},{7,28},{8,1},{9,5},{... | collective-permute-start | bytes 786440 | tf_op jit(solution)/shard_map/ppermute | solution.py:93
  19.0 0.7 copy-start.4
  25.2 1.6 copy-start.6
  26.1 14.4 %copy-start.5 = (s32[256]{0:T(256)S(1)}, s32[256]{0:T(256)}, u32[]{:S(2)}) copy-start(s32[256]{0:T(256)} %param.13) | copy-start | bytes 3076
  28.2 41.2 %all-to-all-start.2 = ((bf16[8,64,512]{2,1,0:T(8,128)(2,1)}), bf16[8,64,512]{2,1,0:T(8,128)(2,1)S(1)}, u32[]{:S(2)}, u32[]{:S(2)}) async-start(bf16[8,64,512]{2,1,0:T(8,128)(2,1)} %bitcast.63), calls=%async_computation.2 | async-start | bytes 1048576 | tf_op jit(solution)/shard_map/all_to_all | solution.py:78
  41.4 34.6 %copy-start.7 = (s32[256]{0:T(256)}, s32[256]{0:T(256)S(1)}, u32[]{:S(2)}) copy-start(s32[256]{0:T(256)S(1)} %multiply_add_fusion) | copy-start | bytes 3076
  73.0 3.0 %copy-start.1 = (bf16[2048,512]{1,0:T(8,128)(2,1)S(1)}, bf16[2048,512]{1,0:T(8,128)(2,1)}, u32[]{:S(2)}) copy-start(bf16[2048,512]{1,0:T(8,128)(2,1)} %all-gather.2.cloned.1.call-done) | copy-start | bytes 6291460
  73.0 3.0 %copy-start.3 = (bf16[256,2048]{1,0:T(8,128)(2,1)S(1)}, bf16[256,2048]{1,0:T(8,128)(2,1)}, u32[]{:S(2)}) copy-start(bf16[256,2048]{1,0:T(8,128)(2,1)} %param.9) | copy-start | bytes 3145732
  77.8 19.7 %all-to-all-start = ((bf16[4,768,128]{2,1,0:T(8,128)(2,1)}), bf16[4,768,128]{2,1,0:T(8,128)(2,1)S(1)}, u32[]{:S(2)}, u32[]{:S(2)}) async-start(bf16[4,768,128]{2,1,0:T(8,128)(2,1)} %bitcast_bitcast_fusion), calls=%async_computation | async-start | bytes 1572864 | tf_op jit(solution)/shard_map/all_to_all | solution.py:117
  97.4 52.8 %all-to-all-start.3 = ((bf16[8,1024,128]{2,1,0:T(8,128)(2,1)}), bf16[8,1024,128]{2,1,0:T(8,128)(2,1)}, u32[]{:S(2)}, u32[]{:S(2)}) async-start(bf16[8,1024,128]{2,1,0:T(8,128)(2,1)} %bitcast.58), calls=%async_computation.3 | async-start | bytes 4194304 | tf_op jit(solution)/shard_map/all_to_all | solution.py:107
  101.8 3.5 %copy-start.2 = (bf16[2048,512]{1,0:T(8,128)(2,1)S(1)}, bf16[2048,512]{1,0:T(8,128)(2,1)}, u32[]{:S(2)}) copy-start(bf16[2048,512]{1,0:T(8,128)(2,1)} %all-gather.2.cloned.1.call-done) | copy-start | bytes 6291460
  150.3 10.2 %all-to-all-start.1 = ((bf16[8,64,128]{2,1,0:T(8,128)(2,1)}), bf16[8,64,128]{2,1,0:T(8,128)(2,1)S(1)}, u32[]{:S(2)}, u32[]{:S(2)}) async-start(bf16[8,64,128]{2,1,0:T(8,128)(2,1)} %bitcast.6), calls=%async_computation.1 | async-start | bytes 262144 | tf_op jit(solution)/shard_map/all_to_all | solution.py:123
  155.6 29.6 %collective-permute-start.1 = (f32[1024,128]{1,0:T(8,128)S(1)}, f32[1024,128]{1,0:T(8,128)S(1)}, u32[]{:S(2)}, u32[]{:S(2)}) collective-permute-start(f32[1024,128]{1,0:T(8,128)S(1)} %broadcast_multiply_fusion), channel_id=1, source_target_pairs={{0,0},{4,1},{8,2},{12,3},{16,4},{20,5},{24,6},{28,7},{1,8},{5,9},{... | collective-permute-start | bytes 1572872 | tf_op jit(solution)/shard_map/ppermute | solution.py:109
Sparse Core Ops, SparseCore 0:
  19.8 53.1 all-gather.1

commit v2 on v1

--- a/solution.py
+++ b/solution.py
@@ -1,6 +1,8 @@
 import jax
 import jax.numpy as jnp
 from jax import lax
+from jax.experimental import pallas as pl
+from jax.experimental.pallas import tpu as pltpu
 from jax.sharding import PartitionSpec as P
 
 HEAD_DIM = 128
@@ -39,6 +41,81 @@
     before = jnp.cumsum(onehot_marks, axis=0) - onehot_marks
     owner_rank = jnp.sum(before * onehot_marks, axis=1)
     return owners * capacity + owner_rank
+
+
+def share_kernel(text_ref, image_ref, back_ref, image_back_ref, out_ref):
+    contract = (((0,), (0,)), ((), ()))
+    part = lax.dot_general(
+        text_ref[...], back_ref[...], contract, preferred_element_type=jnp.float32
+    ) + lax.dot_general(
+        image_ref[...], image_back_ref[...], contract, preferred_element_type=jnp.float32
+    )
+    part = part.astype(out_ref.dtype)
+    width = out_ref.shape[2]
+    for head in range(out_ref.shape[0]):
+        out_ref[head] = part[:, head * width : (head + 1) * width]
+
+
+def weight_shares(text, image, back, image_back, head_cols):
+    columns = text.shape[1]
+    heads = back.shape[1] // head_cols
+    tile = min(512, columns)
+    return pl.pallas_call(
+        share_kernel,
+        grid=(columns // tile,),
+        in_specs=[
+            pl.BlockSpec((text.shape[0], tile), lambda i: (0, i)),
+            pl.BlockSpec((image.shape[0], tile), lambda i: (0, i)),
+            pl.BlockSpec(back.shape, lambda i: (0, 0)),
+            pl.BlockSpec(image_back.shape, lambda i: (0, 0)),
+        ],
+        out_specs=pl.BlockSpec((heads, tile, head_cols), lambda i: (0, i, 0)),
+        out_shape=jax.ShapeDtypeStruct((heads, columns, head_cols), jnp.bfloat16),
+        cost_estimate=pl.CostEstimate(
+            flops=2 * (text.size + image.size) * back.shape[1],
+            bytes_accessed=2 * (text.size + image.size + columns * back.shape[1]),
+            transcendentals=0,
+        ),
+    )(text, image, back, image_back)
+
+
+def project_kernel(text_ref, image_ref, weight_ref, out_ref):
+    step = pl.program_id(0)
+    last = pl.num_programs(0) - 1
+    rows = jnp.where(step == last, image_ref[...], text_ref[...])
+    part = jnp.dot(rows, weight_ref[...], preferred_element_type=jnp.float32).astype(out_ref.dtype)
+    width = out_ref.shape[2]
+    for head in range(out_ref.shape[0]):
+        out_ref[head] = part[:, head * width : (head + 1) * width]
+
+
+def projection_parts(text, image, weight, head_cols):
+    heads = weight.shape[1] // head_cols
+    tile, columns = image.shape
+    text_tiles = text.shape[0] // tile
+    return pl.pallas_call(
+        project_kernel,
+        grid=(text_tiles + 1,),
+        in_specs=[
+            pl.BlockSpec((tile, columns), lambda i: (jnp.minimum(i, text_tiles - 1), 0)),
+            pl.BlockSpec((tile, columns), lambda i: (0, 0)),
+            pl.BlockSpec(weight.shape, lambda i: (0, 0)),
+        ],
+        out_specs=pl.BlockSpec((heads, tile, head_cols), lambda i: (0, i, 0)),
+        out_shape=jax.ShapeDtypeStruct((heads, text.shape[0] + tile, head_cols), jnp.bfloat16),
+        cost_estimate=pl.CostEstimate(
+            flops=2 * (text.size + image.size) * weight.shape[1],
+            bytes_accessed=2 * (text.size + image.size + weight.size),
+            transcendentals=0,
+        ),
+    )(text, image, weight)
+
+
+def spread(piece, axis):
+    count = lax.axis_size(axis)
+    copies = jnp.broadcast_to(piece[None], (count,) + piece.shape)
+    got = lax.all_to_all(copies, axis, split_axis=0, concat_axis=0, tiled=True)
+    return got.reshape((count * piece.shape[0],) + piece.shape[1:])
 
 
 def per_device(
@@ -91,29 +168,22 @@
             target = (unit % halves) * tp_count + part
             moves.append((unit * tp_count + part, target * tp_count + unit // halves))
     own_piece = lax.ppermute(own_piece, units + ("tp",), moves)
-    weight_rows = lax.all_gather(own_piece, units, axis=0, tiled=True)
-
-    weight_part = lax.dot_general(
-        text_embeds, text_back, (((0,), (0,)), ((), ())), preferred_element_type=jnp.float32
-    )
-    weight_part = (
-        weight_part
-        + lax.dot_general(
-            image_embeds, image_back, (((0,), (0,)), ((), ())), preferred_element_type=jnp.float32
-        )
-    ).astype(jnp.bfloat16)
-    weight_part = weight_part.reshape(halves, weight_block, tp_count, head_cols)
-    weight_part = weight_part.transpose(0, 2, 1, 3).reshape(unit_count, weight_block, head_cols)
-    shares = lax.all_to_all(weight_part, units, split_axis=0, concat_axis=0, tiled=True)
+    weight_rows = spread(spread(own_piece, "fsdp"), "group")
+
+    shares = weight_shares(text_embeds, image_embeds, text_back, image_back, head_cols)
+    shares = shares.reshape(core_count, fsdp_count, weight_block, head_cols)
+    shares = lax.all_to_all(shares, "group", split_axis=0, concat_axis=0, tiled=True)
+    shares = jnp.sum(shares.astype(jnp.float32), axis=0).astype(jnp.bfloat16)
+    shares = lax.all_to_all(shares, "fsdp", split_axis=0, concat_axis=0, tiled=True)
     weight_grad = jnp.sum(shares.astype(jnp.float32), axis=0) / row_count
-    weight_grad = lax.ppermute(weight_grad, units + ("tp",), [(b, a) for a, b in moves])
-
-    text_part = jnp.dot(text_embeds, weight_rows, preferred_element_type=jnp.float32)
-    image_part = jnp.dot(image_embeds, weight_rows, preferred_element_type=jnp.float32)
-    both = jnp.concatenate(
-        [text_part.astype(jnp.bfloat16), image_part.astype(jnp.bfloat16)], axis=0
-    )
-    both = both.reshape(row_count + image_count, tp_count, head_cols).transpose(1, 0, 2)
+    returns = []
+    for unit in range(unit_count):
+        for part in range(tp_count):
+            holder = (unit % halves) + part * halves
+            returns.append((holder * tp_count + unit // halves, unit * tp_count + part))
+    weight_grad = lax.ppermute(weight_grad, units + ("tp",), returns)
+
+    both = projection_parts(text_embeds, image_embeds, weight_rows, head_cols)
     both = lax.all_to_all(both, "tp", split_axis=0, concat_axis=0, tiled=True)
     both = jnp.sum(both.astype(jnp.float32), axis=0)
     image_proj = both[row_count:].astype(jnp.bfloat16)

time: 194 us -> 170 us (0.88)
  the two profiles are of different devices: /device:TPU:4 before, /device:TPU:25 now
where the time goes in v2:
time: 170 us
  waiting for transfers between devices  84 us (49%)
  starting transfers between devices  39.7 us (23%)
  other arithmetic  15.5 us (9%)
  Pallas kernels  10.5 us (6%)
  matrix products  8.26 us (5%)
  blocking collectives  5.98 us (4%)
  local copies, waits for them, and re-layouts  4.85 us (3%)
    ppermute x1, waiting for transfers between devices, per_device(): weight_grad = lax.ppermute(weight_grad, units + ('tp',), returns)  24.3 us
    ppermute x1, waiting for transfers between devices, per_device(): own_piece = lax.ppermute(own_piece, units + ('tp',), moves)  21.9 us
    all_to_all x1, waiting for transfers between devices, per_device(): lax.all_to_all(shares, 'fsdp', split_axis=0, concat_axis=0, tiled=True)  16.1 us
    all_to_all x1, waiting for transfers between devices, spread(): got = lax.all_to_all(copies, axis, split_axis=0, concat_axis=0, tiled=True)  14.3 us
    all_to_all x1, waiting for transfers between devices, per_device(): both = lax.all_to_all(both, 'tp', split_axis=0, concat_axis=0, tiled=True)  7.49 us
    all_to_all x1, starting transfers between devices, per_device(): lax.all_to_all(outgoing.reshape(unit_count, capacity, head_cols), units,...  7.05 us
    all_to_all x1, starting transfers between devices, per_device(): lax.all_to_all(shares, 'fsdp', split_axis=0, concat_axis=0, tiled=True)  6.11 us
    all_to_all x1, blocking collectives, spread(): got = lax.all_to_all(copies, axis, split_axis=0, concat_axis=0, tiled=True)  5.98 us
  transfers between devices with their start and end apart: 8, of which 5 were waited for; matrix products, arithmetic and copies ran while one was open for 10% of the time, Pallas kernels for 6%

profile of v2, /device:TPU:25, one launch (start us, length us, event | category | flops | bytes accessed | tf_op | source)
XLA Modules:
  0.0 169.6 jit_solution(8716335513929672151)
XLA Ops:
  5.6 2.5 %broadcast_select_fusion = (bf16[512,4,128]{2,1,0:T(4,128)(2,1)}, bf16[512,4,128]{2,1,0:T(4,128)(2,1)S(1)}) fusion(pred[512]{0:T(512)(128)(4,1)S(1)} %broadcast_compare_fusion, bf16[512,4,64]{2,1,0:T(4,128)(2,1)S(1)} %get-tuple-element.23, bf16[512,4,64]{2,1,0:T(4,128)(2,1)S(1)} %get-tuple-element.22), kind=kLoop, calls=%fused_computation.22 | loop fusion | flops 1310720 | bytes 1573376 | tf_op jit(solution)/shard_map/jit(_where)/select_n | solution.py:148
  8.2 1.4 convolution_convert_fusion.2
  9.5 5.4 %all-to-all-start.4 = ((bf16[8,64,512]{2,1,0:T(8,128)(2,1)}), bf16[8,64,512]{2,1,0:T(8,128)(2,1)S(1)}, u32[]{:S(2)}, u32[]{:S(2)}) async-start(bf16[8,64,512]{2,1,0:T(8,128)(2,1)} %bitcast.9), calls=%async_computation.4 | async-start | bytes 1048576 | tf_op jit(solution)/shard_map/all_to_all | solution.py:155
  14.9 3.9 %collective-permute-start = (bf16[256,512]{1,0:T(8,128)(2,1)S(1)}, bf16[256,512]{1,0:T(8,128)(2,1)S(1)}, u32[]{:S(2)}, u32[]{:S(2)}) collective-permute-start(bf16[256,512]{1,0:T(8,128)(2,1)S(1)} %constant_dynamic-slice_fusion), channel_id=1, source_target_pairs={{0,0},{1,4},{2,8},{3,12},{4,16},{5,20},{6,24},{7,28},{8,1},{9,5},{... | collective-permute-start | bytes 786440 | tf_op jit(solution)/shard_map/ppermute | solution.py:170
  18.8 21.9 %collective-permute-done = bf16[256,512]{1,0:T(8,128)(2,1)S(1)} collective-permute-done((bf16[256,512]{1,0:T(8,128)(2,1)S(1)}, bf16[256,512]{1,0:T(8,128)(2,1)S(1)}, u32[]{:S(2)}, u32[]{:S(2)}) %collective-permute-start) | collective-permute-done | bytes 262176 | tf_op jit(solution)/shard_map/ppermute | solution.py:170
  41.8 5.6 %all-to-all-start = ((bf16[4,256,512]{2,1,0:T(8,128)(2,1)}), bf16[4,256,512]{2,1,0:T(8,128)(2,1)S(1)}, u32[]{:S(2)}, u32[]{:S(2)}) async-start(bf16[4,256,512]{2,1,0:T(8,128)(2,1)} %broadcast_in_dim.38), calls=%async_computation | async-start | bytes 2097152 | tf_op jit(solution)/shard_map/all_to_all | solution.py:117
  50.3 5.4 %shard_map.112 = bf16[4,2048,128]{2,1,0:T(8,128)(2,1)} custom-call(bf16[512,2048]{1,0:T(8,128)(2,1)} %text_ref.3, bf16[256,2048]{1,0:T(8,128)(2,1)} %image_ref.3, bf16[512,512]{1,0:T(8,128)(2,1)} %bitcast_select_fusion.back_ref, bf16[256,512]{1,0:T(8,128)(2,1)} %convolution_convert_fusion.3.image_back_ref), custom_call_target="tpu_custom_call" | custom-call | flops 1610612736 | bytes 5242880 | tf_op jit(solution)/shard_map/pallas_call | solution.py:63
  55.7 14.3 %all-to-all-done = bf16[4,256,512]{2,1,0:T(8,128)(2,1)S(1)} async-done(((bf16[4,256,512]{2,1,0:T(8,128)(2,1)}), bf16[4,256,512]{2,1,0:T(8,128)(2,1)S(1)}, u32[]{:S(2)}, u32[]{:S(2)}) %all-to-all-start) | async-done | bytes 1048608 | tf_op jit(solution)/shard_map/all_to_all | solution.py:117
  70.1 6.0 %all_to_all.35 = bf16[2,1024,512]{2,1,0:T(8,128)(2,1)} all-to-all(bf16[2,1024,512]{2,1,0:T(8,128)(2,1)S(1)} %broadcast_in_dim.40), channel_id=1, replica_groups=mesh['group'=2,'fsdp'=4,'tp'=4] {'group'}, dimensions={0} | all-to-all | bytes 4194304 | tf_op jit(solution)/shard_map/all_to_all | solution.py:117
  76.1 4.1 %all-to-all-start.5 = ((bf16[2,4,1024,128]{3,2,1,0:T(8,128)(2,1)}), bf16[2,4,1024,128]{3,2,1,0:T(8,128)(2,1)S(1)}, u32[]{:S(2)}, u32[]{:S(2)}) async-start(bf16[2,4,1024,128]{3,2,1,0:T(8,128)(2,1)} %bitcast.11), calls=%async_computation.5 | async-start | bytes 4194304 | tf_op jit(solution)/shard_map/all_to_all | solution.py:175
  80.2 5.1 %shard_map.111 = bf16[4,768,128]{2,1,0:T(8,128)(2,1)} custom-call(bf16[512,2048]{1,0:T(8,128)(2,1)} %text_ref.3, bf16[256,2048]{1,0:T(8,128)(2,1)} %image_ref.3, bf16[2048,512]{1,0:T(8,128)(2,1)} %bitcast.38), custom_call_target="tpu_custom_call" | custom-call | flops 1610612736 | bytes 5242880 | tf_op jit(solution)/shard_map/pallas_call | solution.py:96
  85.3 1.3 copy-done.2
  86.6 4.2 %all-to-all-start.2 = ((bf16[4,768,128]{2,1,0:T(8,128)(2,1)}), bf16[4,768,128]{2,1,0:T(8,128)(2,1)}, u32[]{:S(2)}, u32[]{:S(2)}) async-start(bf16[4,768,128]{2,1,0:T(8,128)(2,1)} %shard_map.111), calls=%async_computation.2 | async-start | bytes 1572864 | tf_op jit(solution)/shard_map/all_to_all | solution.py:187
  90.9 3.4 %reduce_sum.51 = bf16[4,1024,128]{2,1,0:T(8,128)(2,1)} reduce(bf16[2,4,1024,128]{3,2,1,0:T(8,128)(2,1)} %copy-done.2, bf16[]{:T(256)} %constant.62.clone.1), dimensions={0}, to_apply=%region_5.6 | reduce | flops 524288 | bytes 3145730 | tf_op jit(solution)/shard_map/reduce_sum | solution.py:176
  94.3 7.5 %all-to-all-done.2 = bf16[4,768,128]{2,1,0:T(8,128)(2,1)} async-done(((bf16[4,768,128]{2,1,0:T(8,128)(2,1)}), bf16[4,768,128]{2,1,0:T(8,128)(2,1)}, u32[]{:S(2)}, u32[]{:S(2)}) %all-to-all-start.2) | async-done | bytes 786464 | tf_op jit(solution)/shard_map/all_to_all | solution.py:187
  101.8 6.1 %all-to-all-start.6 = ((bf16[4,1024,128]{2,1,0:T(8,128)(2,1)}), bf16[4,1024,128]{2,1,0:T(8,128)(2,1)}, u32[]{:S(2)}, u32[]{:S(2)}) async-start(bf16[4,1024,128]{2,1,0:T(8,128)(2,1)} %reduce_sum.51), calls=%async_computation.6 | async-start | bytes 2097152 | tf_op jit(solution)/shard_map/all_to_all | solution.py:177
  107.9 1.7 %convolution_convert_fusion.1 = bf16[256,2048]{1,0:T(8,128)(2,1)} fusion(bf16[256,512]{1,0:T(8,128)(2,1)S(1)} %copy-done.3, bf16[2048,512]{1,0:T(8,128)(2,1)S(1)} %bitcast.39), kind=kOutput, calls=%fused_computation.1 | convolution fusion | flops 537395200 | bytes 3407872 | tf_op jit(solution)/shard_map/dot_general | solution.py:205
  109.6 2.6 %convolution_convert_fusion = bf16[512,2048]{1,0:T(8,128)(2,1)} fusion(bf16[2048,512]{1,0:T(8,128)(2,1)S(1)} %bitcast.40, bf16[64,8,4,128]{3,2,1,0:T(4,128)(2,1)S(1)} %bitcast.44), kind=kOutput, calls=%fused_computation | convolution fusion | flops 1074790400 | bytes 4718592 | tf_op jit(solution)/shard_map/dot_general | solution.py:202
  112.2 1.3 convert_reduce_fusion.1
  114.8 16.1 %all-to-all-done.6 = bf16[4,1024,128]{2,1,0:T(8,128)(2,1)} async-done(((bf16[4,1024,128]{2,1,0:T(8,128)(2,1)}), bf16[4,1024,128]{2,1,0:T(8,128)(2,1)}, u32[]{:S(2)}, u32[]{:S(2)}) %all-to-all-start.6) | async-done | bytes 1048608 | tf_op jit(solution)/shard_map/all_to_all | solution.py:177
  130.8 7.0 %all-to-all-start.3 = ((bf16[8,64,128]{2,1,0:T(8,128)(2,1)}), bf16[8,64,128]{2,1,0:T(8,128)(2,1)S(1)}, u32[]{:S(2)}, u32[]{:S(2)}) async-start(bf16[8,64,128]{2,1,0:T(8,128)(2,1)} %bitcast.5), calls=%async_computation.3 | async-start | bytes 262144 | tf_op jit(solution)/shard_map/all_to_all | solution.py:193
  137.9 1.4 convert_reduce_fusion
  139.3 3.3 %collective-permute-start.1 = (f32[1024,128]{1,0:T(8,128)S(1)}, f32[1024,128]{1,0:T(8,128)S(1)}, u32[]{:S(2)}, u32[]{:S(2)}) collective-permute-start(f32[1024,128]{1,0:T(8,128)S(1)} %broadcast_multiply_fusion), channel_id=1, source_target_pairs={{0,0},{8,1},{16,2},{24,3},{4,4},{12,5},{20,6},{28,7},{1,8},{9,9},{... | collective-permute-start | bytes 1572872 | tf_op jit(solution)/shard_map/ppermute | solution.py:184
  144.5 24.3 %collective-permute-done.1 = f32[1024,128]{1,0:T(8,128)S(1)} collective-permute-done((f32[1024,128]{1,0:T(8,128)S(1)}, f32[1024,128]{1,0:T(8,128)S(1)}, u32[]{:S(2)}, u32[]{:S(2)}) %collective-permute-start.1) | collective-permute-done | bytes 524320 | tf_op jit(solution)/shard_map/ppermute | solution.py:184
  (49 shorter events, 12.9 us)
Async XLA Ops:
  0.6 14.3 %copy-start = (bf16[1024,512]{1,0:T(8,128)(2,1)S(1)}, bf16[1024,512]{1,0:T(8,128)(2,1)}, u32[]{:S(2)}) copy-start(bf16[1024,512]{1,0:T(8,128)(2,1)} %param.10) | copy-start | bytes 3145732
  4.7 3.4 %copy-start.6 = (s32[512]{0:T(512)S(1)}, s32[512]{0:T(512)}, u32[]{:S(2)}) copy-start(s32[512]{0:T(512)} %param.14) | copy-start | bytes 6148
  9.5 31.2 %all-to-all-start.4 = ((bf16[8,64,512]{2,1,0:T(8,128)(2,1)}), bf16[8,64,512]{2,1,0:T(8,128)(2,1)S(1)}, u32[]{:S(2)}, u32[]{:S(2)}) async-start(bf16[8,64,512]{2,1,0:T(8,128)(2,1)} %bitcast.9), calls=%async_computation.4 | async-start | bytes 1048576 | tf_op jit(solution)/shard_map/all_to_all | solution.py:155
  14.9 32.4 %copy-start.5 = (s32[256]{0:T(256)S(1)}, s32[256]{0:T(256)}, u32[]{:S(2)}) copy-start(s32[256]{0:T(256)} %param.13) | copy-start | bytes 3076
  14.9 25.8 %collective-permute-start = (bf16[256,512]{1,0:T(8,128)(2,1)S(1)}, bf16[256,512]{1,0:T(8,128)(2,1)S(1)}, u32[]{:S(2)}, u32[]{:S(2)}) collective-permute-start(bf16[256,512]{1,0:T(8,128)(2,1)S(1)} %constant_dynamic-slice_fusion), channel_id=1, source_target_pairs={{0,0},{1,4},{2,8},{3,12},{4,16},{5,20},{6,24},{7,28},{8,1},{9,5},{... | collective-permute-start | bytes 786440 | tf_op jit(solution)/shard_map/ppermute | solution.py:170
  41.8 28.2 %all-to-all-start = ((bf16[4,256,512]{2,1,0:T(8,128)(2,1)}), bf16[4,256,512]{2,1,0:T(8,128)(2,1)S(1)}, u32[]{:S(2)}, u32[]{:S(2)}) async-start(bf16[4,256,512]{2,1,0:T(8,128)(2,1)} %broadcast_in_dim.38), calls=%async_computation | async-start | bytes 2097152 | tf_op jit(solution)/shard_map/all_to_all | solution.py:117
  76.1 9.2 %all-to-all-start.5 = ((bf16[2,4,1024,128]{3,2,1,0:T(8,128)(2,1)}), bf16[2,4,1024,128]{3,2,1,0:T(8,128)(2,1)S(1)}, u32[]{:S(2)}, u32[]{:S(2)}) async-start(bf16[2,4,1024,128]{3,2,1,0:T(8,128)(2,1)} %bitcast.11), calls=%async_computation.5 | async-start | bytes 4194304 | tf_op jit(solution)/shard_map/all_to_all | solution.py:175
  85.3 1.3 copy-start.2
  86.6 15.1 %all-to-all-start.2 = ((bf16[4,768,128]{2,1,0:T(8,128)(2,1)}), bf16[4,768,128]{2,1,0:T(8,128)(2,1)}, u32[]{:S(2)}, u32[]{:S(2)}) async-start(bf16[4,768,128]{2,1,0:T(8,128)(2,1)} %shard_map.111), calls=%async_computation.2 | async-start | bytes 1572864 | tf_op jit(solution)/shard_map/all_to_all | solution.py:187
  90.8 17.0 %copy-start.1 = (bf16[2,1024,512]{2,1,0:T(8,128)(2,1)S(1)}, bf16[2,1024,512]{2,1,0:T(8,128)(2,1)}, u32[]{:S(2)}) copy-start(bf16[2,1024,512]{2,1,0:T(8,128)(2,1)} %all_to_all.35) | copy-start | bytes 6291460
  90.8 17.0 %copy-start.3 = (bf16[256,512]{1,0:T(8,128)(2,1)S(1)}, bf16[256,512]{1,0:T(8,128)(2,1)}, u32[]{:S(2)}) copy-start(bf16[256,512]{1,0:T(8,128)(2,1)} %convolution_convert_fusion.3.image_back_ref) | copy-start | bytes 786436
  101.8 29.1 %all-to-all-start.6 = ((bf16[4,1024,128]{2,1,0:T(8,128)(2,1)}), bf16[4,1024,128]{2,1,0:T(8,128)(2,1)}, u32[]{:S(2)}, u32[]{:S(2)}) async-start(bf16[4,1024,128]{2,1,0:T(8,128)(2,1)} %reduce_sum.51), calls=%async_computation.6 | async-start | bytes 2097152 | tf_op jit(solution)/shard_map/all_to_all | solution.py:177
  107.9 1.7 %copy-start.4 = (bf16[512,4,128]{2,1,0:T(4,128)(2,1)S(1)}, bf16[512,4,128]{2,1,0:T(4,128)(2,1)}, u32[]{:S(2)}) copy-start(bf16[512,4,128]{2,1,0:T(4,128)(2,1)} %get-tuple-element.20) | copy-start | bytes 1572868
  113.5 29.2 %copy-start.7 = (f32[128]{0:T(128)S(1)}, f32[128]{0:T(128)}, u32[]{:S(2)}) copy-start(f32[128]{0:T(128)} %param.11) | copy-start | bytes 1540
  130.8 11.9 %all-to-all-start.3 = ((bf16[8,64,128]{2,1,0:T(8,128)(2,1)}), bf16[8,64,128]{2,1,0:T(8,128)(2,1)S(1)}, u32[]{:S(2)}, u32[]{:S(2)}) async-start(bf16[8,64,128]{2,1,0:T(8,128)(2,1)} %bitcast.5), calls=%async_computation.3 | async-start | bytes 262144 | tf_op jit(solution)/shard_map/all_to_all | solution.py:193
  139.3 29.5 %collective-permute-start.1 = (f32[1024,128]{1,0:T(8,128)S(1)}, f32[1024,128]{1,0:T(8,128)S(1)}, u32[]{:S(2)}, u32[]{:S(2)}) collective-permute-start(f32[1024,128]{1,0:T(8,128)S(1)} %broadcast_multiply_fusion), channel_id=1, source_target_pairs={{0,0},{8,1},{16,2},{24,3},{4,4},{12,5},{20,6},{28,7},{1,8},{9,9},{... | collective-permute-start | bytes 1572872 | tf_op jit(solution)/shard_map/ppermute | solution.py:184

commit v3 on v2

--- a/solution.py
+++ b/solution.py
@@ -118,6 +118,33 @@
     return got.reshape((count * piece.shape[0],) + piece.shape[1:])
 
 
+def shifted(values, axis, step):
+    count = lax.axis_size(axis)
+    return lax.ppermute(values, axis, [(i, (i + step) % count) for i in range(count)])
+
+
+def exchange_sum(blocks, axis):
+    count = lax.axis_size(axis)
+    me = lax.axis_index(axis)
+    total = lax.dynamic_index_in_dim(blocks, me, 0, keepdims=False).astype(jnp.float32)
+    for step in range(1, count):
+        block = lax.dynamic_index_in_dim(blocks, (me + step) % count, 0, keepdims=False)
+        total = total + shifted(block, axis, step).astype(jnp.float32)
+    return total
+
+
+def share_rows(piece, axis):
+    count = lax.axis_size(axis)
+    me = lax.axis_index(axis)
+    rows = piece.shape[0]
+    full = jnp.zeros((count * rows,) + piece.shape[1:], piece.dtype)
+    full = lax.dynamic_update_slice_in_dim(full, piece, me * rows, 0)
+    for step in range(1, count):
+        source = (me + count - step) % count
+        full = lax.dynamic_update_slice_in_dim(full, shifted(piece, axis, step), source * rows, 0)
+    return full
+
+
 def per_device(
     text_embeds, image_embeds, key_weight, key_bias, key_cot, image_owner, image_slot, seq_lengths
 ):
@@ -168,12 +195,12 @@
             target = (unit % halves) * tp_count + part
             moves.append((unit * tp_count + part, target * tp_count + unit // halves))
     own_piece = lax.ppermute(own_piece, units + ("tp",), moves)
-    weight_rows = spread(spread(own_piece, "fsdp"), "group")
+    chip_rows = spread(own_piece, "fsdp")
 
     shares = weight_shares(text_embeds, image_embeds, text_back, image_back, head_cols)
     shares = shares.reshape(core_count, fsdp_count, weight_block, head_cols)
-    shares = lax.all_to_all(shares, "group", split_axis=0, concat_axis=0, tiled=True)
-    shares = jnp.sum(shares.astype(jnp.float32), axis=0).astype(jnp.bfloat16)
+    shares = exchange_sum(shares, "group").astype(jnp.bfloat16)
+    shares, chip_rows = lax.optimization_barrier((shares, chip_rows))
     shares = lax.all_to_all(shares, "fsdp", split_axis=0, concat_axis=0, tiled=True)
     weight_grad = jnp.sum(shares.astype(jnp.float32), axis=0) / row_count
     returns = []
@@ -183,9 +210,9 @@
             returns.append((holder * tp_count + unit // halves, unit * tp_count + part))
     weight_grad = lax.ppermute(weight_grad, units + ("tp",), returns)
 
+    weight_rows = share_rows(chip_rows, "group")
     both = projection_parts(text_embeds, image_embeds, weight_rows, head_cols)
-    both = lax.all_to_all(both, "tp", split_axis=0, concat_axis=0, tiled=True)
-    both = jnp.sum(both.astype(jnp.float32), axis=0)
+    both = exchange_sum(both, "tp")
     image_proj = both[row_count:].astype(jnp.bfloat16)
     outgoing = lax.dot_general(
         pick, image_proj, (((0,), (0,)), ((), ())), preferred_element_type=jnp.float32

time: 170 us -> 137 us (0.81); the launches traced: 170 us -> 135 us
  waiting for transfers between devices: 84 us -> 55.9 us
  blocking collectives: 5.98 us -> 0 us
  starting transfers between devices: 39.7 us -> 34 us
  local copies, waits for them, and re-layouts: 4.85 us -> 10.2 us
  other arithmetic: 15.5 us -> 13.3 us
  matrix products: 8.26 us -> 10.1 us
    all_to_all x1, waiting for transfers between devices: 16.1 us -> 0.01 us  [per_device(): lax.all_to_all(shares, 'fsdp', split_axis=0, concat_axis=0, tiled=True)]
    all_to_all x2 -> x0, starting transfers between devices: 8.31 us -> none  [the longest x1 4.18 us: per_device(): both = lax.all_to_all(both, 'tp', split_axis=0, concat_axis=0, tiled=True)]
    all_to_all x2 -> x0, waiting for transfers between devices: 7.49 us -> none  [the longest x1 7.49 us: per_device(): both = lax.all_to_all(both, 'tp', split_axis=0, concat_axis=0, tiled=True)]
    ppermute x0 -> x5, waiting for transfers between devices: none -> 6.19 us  [shifted(): lax.ppermute(values, axis, [(i, (i + step) % count) for i in range(count)])]
    all_to_all x1 -> x0, blocking collectives: 5.98 us -> none  [spread(): got = lax.all_to_all(copies, axis, split_axis=0, concat_axis=0, tiled=True)]
    all_to_all x1, waiting for transfers between devices: 14.3 us -> 8.37 us  [spread(): got = lax.all_to_all(copies, axis, split_axis=0, concat_axis=0, tiled=True)]
    reduce_sum x2 -> x0, other arithmetic: 4.7 us -> none  [the longest x1 3.42 us: per_device(): shares = jnp.sum(shares.astype(jnp.float32), axis=0).astype(jnp.bfloat16)]
    squeeze x0 -> x2, local copies, waits for them, and re-layouts: none -> 3.58 us  [exchange_sum(): lax.dynamic_index_in_dim(blocks, (me + step) % count, 0, keepdims=False)]
  transfers between devices with their start and end apart: 8 -> 11, of which waited for: 5 -> 5; matrix products, arithmetic and copies ran while one was open for 10% -> 18% of each run, Pallas kernels for 6% -> 8%
where the time goes in v3:
time: 137 us; the launch traced here: 135 us
  waiting for transfers between devices  55.9 us (41%)
  starting transfers between devices  34 us (25%)
  other arithmetic  13.3 us (10%)
  Pallas kernels  10.5 us (8%)
  local copies, waits for them, and re-layouts  10.2 us (7%)
  matrix products  10.1 us (7%)
    ppermute x1, waiting for transfers between devices, per_device(): weight_grad = lax.ppermute(weight_grad, units + ('tp',), returns)  21.4 us
    ppermute x1, waiting for transfers between devices, per_device(): own_piece = lax.ppermute(own_piece, units + ('tp',), moves)  19.9 us
    all_to_all x1, waiting for transfers between devices, spread(): got = lax.all_to_all(copies, axis, split_axis=0, concat_axis=0, tiled=True)  8.37 us
    all_to_all x1, starting transfers between devices, spread(): got = lax.all_to_all(copies, axis, split_axis=0, concat_axis=0, tiled=True)  6.31 us
    ppermute x5, waiting for transfers between devices, shifted(): lax.ppermute(values, axis, [(i, (i + step) % count) for i in range(count)])  6.19 us
    all_to_all x1, starting transfers between devices, per_device(): lax.all_to_all(returning.reshape(unit_count, capacity, key_cols), units,...  5.37 us
    all_to_all x1, starting transfers between devices, per_device(): lax.all_to_all(shares, 'fsdp', split_axis=0, concat_axis=0, tiled=True)  5.36 us
    pallas_call x1, Pallas kernels, weight_shares(): pl.pallas_call(share_kernel, grid=(columns // tile,), in_specs=[pl.BlockS...  5.36 us
  transfers between devices with their start and end apart: 11, of which 5 were waited for; matrix products, arithmetic and copies ran while one was open for 18% of the time, Pallas kernels for 8%

profile of v3, /device:TPU:25, one launch (start us, length us, event | category | flops | bytes accessed | tf_op | source)
XLA Modules:
  0.0 134.9 jit_solution(12772641685637158837)
XLA Ops:
  5.7 1.4 %convolution_convert_fusion.2 = bf16[512,512]{1,0:T(8,128)(2,1)} fusion(s32[512]{0:T(512)S(1)} %copy-done.6, bf16[64,8,4,128]{3,2,1,0:T(4,128)(2,1)S(1)} %bitcast.50), kind=kOutput, calls=%fused_computation.5 | convolution fusion | flops 268959744 | bytes 1050624 | tf_op jit(solution)/shard_map/dot_general | solution.py:179
  7.0 5.4 %all-to-all-start = ((bf16[8,64,512]{2,1,0:T(8,128)(2,1)}), bf16[8,64,512]{2,1,0:T(8,128)(2,1)S(1)}, u32[]{:S(2)}, u32[]{:S(2)}) async-start(bf16[8,64,512]{2,1,0:T(8,128)(2,1)} %bitcast.3), calls=%async_computation | async-start | bytes 1048576 | tf_op jit(solution)/shard_map/all_to_all | solution.py:182
  12.4 3.9 %collective-permute-start.1 = (bf16[256,512]{1,0:T(8,128)(2,1)S(1)}, bf16[256,512]{1,0:T(8,128)(2,1)S(1)}, u32[]{:S(2)}, u32[]{:S(2)}) collective-permute-start(bf16[256,512]{1,0:T(8,128)(2,1)S(1)} %constant_dynamic-slice_fusion), channel_id=1, source_target_pairs={{0,0},{1,4},{2,8},{3,12},{4,16},{5,20},{6,24},{7,28},{8,1},{9,5},{... | collective-permute-start | bytes 786440 | tf_op jit(solution)/shard_map/ppermute | solution.py:197
  18.3 19.9 %collective-permute-done.1 = bf16[256,512]{1,0:T(8,128)(2,1)S(1)} collective-permute-done((bf16[256,512]{1,0:T(8,128)(2,1)S(1)}, bf16[256,512]{1,0:T(8,128)(2,1)S(1)}, u32[]{:S(2)}, u32[]{:S(2)}) %collective-permute-start.1) | collective-permute-done | bytes 262176 | tf_op jit(solution)/shard_map/ppermute | solution.py:197
  39.3 6.3 %all-to-all-start.1 = ((bf16[4,256,512]{2,1,0:T(8,128)(2,1)}), bf16[4,256,512]{2,1,0:T(8,128)(2,1)}, u32[]{:S(2)}, u32[]{:S(2)}) async-start(bf16[4,256,512]{2,1,0:T(8,128)(2,1)} %broadcast_in_dim.37), calls=%async_computation.1 | async-start | bytes 2097152 | tf_op jit(solution)/shard_map/all_to_all | solution.py:117
  46.6 5.4 %shard_map.111 = bf16[4,2048,128]{2,1,0:T(8,128)(2,1)} custom-call(bf16[512,2048]{1,0:T(8,128)(2,1)} %text_ref.3, bf16[256,2048]{1,0:T(8,128)(2,1)} %image_ref.3, bf16[512,512]{1,0:T(8,128)(2,1)} %bitcast_select_fusion.back_ref, bf16[256,512]{1,0:T(8,128)(2,1)} %convolution_convert_fusion.3.image_back_ref), custom_call_target="tpu_custom_call" | custom-call | flops 1610612736 | bytes 5242880 | tf_op jit(solution)/shard_map/pallas_call | solution.py:63
  52.0 2.4 %dynamic-slice_bitcast_fusion = bf16[4,1024,128]{2,1,0:T(8,128)(2,1)} fusion(bf16[2,4,1024,128]{3,2,1,0:T(8,128)(2,1)} %bitcast.48, s32[]{:T(128)S(6)} %select_n.108), kind=kLoop, calls=%fused_computation.8 | loop fusion | bytes 2097156 | tf_op jit(solution)/shard_map/jit(dynamic_index_in_dim)/squeeze | solution.py:131
  54.4 3.0 %collective-permute-done = bf16[4,1024,128]{2,1,0:T(8,128)(2,1)} collective-permute-done((bf16[4,1024,128]{2,1,0:T(8,128)(2,1)}, bf16[4,1024,128]{2,1,0:T(8,128)(2,1)}, u32[]{:S(2)}, u32[]{:S(2)}) %collective-permute-start) | collective-permute-done | bytes 1048608 | tf_op jit(solution)/shard_map/ppermute | solution.py:123
  57.4 2.5 %fusion = bf16[4,1024,128]{2,1,0:T(8,128)(2,1)} fusion(bf16[4,1024,128]{2,1,0:T(8,128)(2,1)} %collective-permute-done, bf16[2,4,1024,128]{3,2,1,0:T(8,128)(2,1)S(1)} %bitcast.49, s32[]{:T(128)S(6)} %select_n.106), kind=kLoop, calls=%fused_computation.3 | loop fusion | flops 2097152 | bytes 3145732 | tf_op jit(solution)/shard_map/convert_element_type | solution.py:202
  59.9 8.4 %all-to-all-done.1 = bf16[4,256,512]{2,1,0:T(8,128)(2,1)} async-done(((bf16[4,256,512]{2,1,0:T(8,128)(2,1)}), bf16[4,256,512]{2,1,0:T(8,128)(2,1)}, u32[]{:S(2)}, u32[]{:S(2)}) %all-to-all-start.1) | async-done | bytes 1048608 | tf_op jit(solution)/shard_map/all_to_all | solution.py:117
  68.3 5.4 %all-to-all-start.3 = ((bf16[4,1024,128]{2,1,0:T(8,128)(2,1)}), bf16[4,1024,128]{2,1,0:T(8,128)(2,1)}, u32[]{:S(2)}, u32[]{:S(2)}) async-start(bf16[4,1024,128]{2,1,0:T(8,128)(2,1)} %fusion), calls=%async_computation.3 | async-start | bytes 2097152 | tf_op jit(solution)/shard_map/all_to_all | solution.py:204
  73.8 1.3 constant_dynamic-update-slice_fusion.1
  75.1 1.3 constant_dynamic-update-slice_fusion.weight_ref
  76.5 1.3 copy-done.1
  77.8 5.1 %shard_map.112 = bf16[4,768,128]{2,1,0:T(8,128)(2,1)} custom-call(bf16[512,2048]{1,0:T(8,128)(2,1)} %text_ref.3, bf16[256,2048]{1,0:T(8,128)(2,1)} %image_ref.3, bf16[2048,512]{1,0:T(8,128)(2,1)} %copy-done.1), custom_call_target="tpu_custom_call" | custom-call | flops 1610612736 | bytes 5242880 | tf_op jit(solution)/shard_map/pallas_call | solution.py:96
  84.2 3.2 %collective-permute-start.4 = (bf16[768,128]{1,0:T(8,128)(2,1)S(1)}, bf16[768,128]{1,0:T(8,128)(2,1)S(1)}, u32[]{:S(2)}, u32[]{:S(2)}) collective-permute-start(bf16[768,128]{1,0:T(8,128)(2,1)S(1)} %get-tuple-element.12), channel_id=1, source_target_pairs={{0,2},{1,3},{2,0},{3,1},{4,6},{5,7},{6,4},{7,5},{8,10},{9,11},{10,... | collective-permute-start | bytes 589832 | tf_op jit(solution)/shard_map/ppermute | solution.py:123
  87.4 4.5 %convolution_convert_fusion = bf16[512,2048]{1,0:T(8,128)(2,1)} fusion(bf16[512,512]{1,0:T(8,128)(2,1)} %bitcast_select_fusion.back_ref, bf16[2048,512]{1,0:T(8,128)(2,1)} %copy-done.1), kind=kOutput, calls=%fused_computation | convolution fusion | flops 1074790400 | bytes 4718592 | tf_op jit(solution)/shard_map/dot_general | solution.py:229
  91.9 1.7 %convolution_convert_fusion.1 = bf16[256,2048]{1,0:T(8,128)(2,1)} fusion(bf16[256,512]{1,0:T(8,128)(2,1)S(1)} %copy-done.4, bf16[2048,512]{1,0:T(8,128)(2,1)S(1)} %copy-done.2), kind=kOutput, calls=%fused_computation.1 | convolution fusion | flops 537395200 | bytes 3407872 | tf_op jit(solution)/shard_map/dot_general | solution.py:232
  93.6 3.2 %collective-permute-done.4 = bf16[768,128]{1,0:T(8,128)(2,1)S(1)} collective-permute-done((bf16[768,128]{1,0:T(8,128)(2,1)S(1)}, bf16[768,128]{1,0:T(8,128)(2,1)S(1)}, u32[]{:S(2)}, u32[]{:S(2)}) %collective-permute-start.4) | collective-permute-done | bytes 196640 | tf_op jit(solution)/shard_map/ppermute | solution.py:123
  98.9 5.1 %all-to-all-start.2 = ((bf16[8,64,128]{2,1,0:T(8,128)(2,1)}), bf16[8,64,128]{2,1,0:T(8,128)(2,1)S(1)}, u32[]{:S(2)}, u32[]{:S(2)}) async-start(bf16[8,64,128]{2,1,0:T(8,128)(2,1)} %bitcast.13), calls=%async_computation.2 | async-start | bytes 262144 | tf_op jit(solution)/shard_map/all_to_all | solution.py:220
  104.0 1.4 %convert_reduce_fusion = f32[1024,128]{1,0:T(8,128)S(1)} fusion(bf16[4,1024,128]{2,1,0:T(8,128)(2,1)} %all-to-all-done.3), kind=kLoop, calls=%fused_computation.4 | loop fusion | flops 917504 | bytes 1572864 | tf_op jit(solution)/shard_map/reduce_sum | solution.py:205
  105.5 4.7 %collective-permute-start.6 = (f32[1024,128]{1,0:T(8,128)S(1)}, f32[1024,128]{1,0:T(8,128)S(1)}, u32[]{:S(2)}, u32[]{:S(2)}) collective-permute-start(f32[1024,128]{1,0:T(8,128)S(1)} %broadcast_multiply_fusion), channel_id=1, source_target_pairs={{0,0},{8,1},{16,2},{24,3},{4,4},{12,5},{20,6},{28,7},{1,8},{9,9},{... | collective-permute-start | bytes 1572872 | tf_op jit(solution)/shard_map/ppermute | solution.py:211
  110.6 1.2 fusion.12
  112.7 21.4 %collective-permute-done.6 = f32[1024,128]{1,0:T(8,128)S(1)} collective-permute-done((f32[1024,128]{1,0:T(8,128)S(1)}, f32[1024,128]{1,0:T(8,128)S(1)}, u32[]{:S(2)}, u32[]{:S(2)}) %collective-permute-start.6) | collective-permute-done | bytes 524320 | tf_op jit(solution)/shard_map/ppermute | solution.py:211
  (54 shorter events, 14.5 us)
Async XLA Ops:
  0.6 11.8 %copy-start = (bf16[1024,512]{1,0:T(8,128)(2,1)S(1)}, bf16[1024,512]{1,0:T(8,128)(2,1)}, u32[]{:S(2)}) copy-start(bf16[1024,512]{1,0:T(8,128)(2,1)} %param.10) | copy-start | bytes 3145732
  4.0 1.6 %copy-start.6 = (s32[512]{0:T(512)S(1)}, s32[512]{0:T(512)}, u32[]{:S(2)}) copy-start(s32[512]{0:T(512)} %param.14) | copy-start | bytes 6148
  4.9 11.4 %copy-start.5 = (s32[256]{0:T(256)S(1)}, s32[256]{0:T(256)}, u32[]{:S(2)}) copy-start(s32[256]{0:T(256)} %param.13) | copy-start | bytes 3076
  7.0 31.2 %all-to-all-start = ((bf16[8,64,512]{2,1,0:T(8,128)(2,1)}), bf16[8,64,512]{2,1,0:T(8,128)(2,1)S(1)}, u32[]{:S(2)}, u32[]{:S(2)}) async-start(bf16[8,64,512]{2,1,0:T(8,128)(2,1)} %bitcast.3), calls=%async_computation | async-start | bytes 1048576 | tf_op jit(solution)/shard_map/all_to_all | solution.py:182
  12.4 25.8 %collective-permute-start.1 = (bf16[256,512]{1,0:T(8,128)(2,1)S(1)}, bf16[256,512]{1,0:T(8,128)(2,1)S(1)}, u32[]{:S(2)}, u32[]{:S(2)}) collective-permute-start(bf16[256,512]{1,0:T(8,128)(2,1)S(1)} %constant_dynamic-slice_fusion), channel_id=1, source_target_pairs={{0,0},{1,4},{2,8},{3,12},{4,16},{5,20},{6,24},{7,28},{8,1},{9,5},{... | collective-permute-start | bytes 786440 | tf_op jit(solution)/shard_map/ppermute | solution.py:197
  39.3 29.0 %all-to-all-start.1 = ((bf16[4,256,512]{2,1,0:T(8,128)(2,1)}), bf16[4,256,512]{2,1,0:T(8,128)(2,1)}, u32[]{:S(2)}, u32[]{:S(2)}) async-start(bf16[4,256,512]{2,1,0:T(8,128)(2,1)} %broadcast_in_dim.37), calls=%async_computation.1 | async-start | bytes 2097152 | tf_op jit(solution)/shard_map/all_to_all | solution.py:117
  52.0 5.4 %copy-start.3 = (bf16[4,2048,128]{2,1,0:T(8,128)(2,1)S(1)}, bf16[4,2048,128]{2,1,0:T(8,128)(2,1)}, u32[]{:S(2)}) copy-start(bf16[4,2048,128]{2,1,0:T(8,128)(2,1)} %shard_map.111) | copy-start | bytes 6291460
  54.4 3.0 %collective-permute-start = (bf16[4,1024,128]{2,1,0:T(8,128)(2,1)}, bf16[4,1024,128]{2,1,0:T(8,128)(2,1)}, u32[]{:S(2)}, u32[]{:S(2)}) collective-permute-start(bf16[4,1024,128]{2,1,0:T(8,128)(2,1)} %dynamic-slice_bitcast_fusion), channel_id=1, source_target_pairs={{0,16},{16,0},{1,17},{17,1},{2,18},{18,2},{3,19},{19,3},{4,20},{20... | collective-permute-start | bytes 3145736 | tf_op jit(solution)/shard_map/ppermute | solution.py:123
  68.3 6.8 %collective-permute-start.2 = (bf16[1024,512]{1,0:T(8,128)(2,1)}, bf16[1024,512]{1,0:T(8,128)(2,1)}, u32[]{:S(2)}, u32[]{:S(2)}) collective-permute-start(bf16[1024,512]{1,0:T(8,128)(2,1)} %bitcast.8), channel_id=1, source_target_pairs={{0,16},{16,0},{1,17},{17,1},{2,18},{18,2},{3,19},{19,3},{4,20},{20... | collective-permute-start | bytes 3145736 | tf_op jit(solution)/shard_map/ppermute | solution.py:123
  68.3 30.7 %all-to-all-start.3 = ((bf16[4,1024,128]{2,1,0:T(8,128)(2,1)}), bf16[4,1024,128]{2,1,0:T(8,128)(2,1)}, u32[]{:S(2)}, u32[]{:S(2)}) async-start(bf16[4,1024,128]{2,1,0:T(8,128)(2,1)} %fusion), calls=%async_computation.3 | async-start | bytes 2097152 | tf_op jit(solution)/shard_map/all_to_all | solution.py:204
  76.5 1.3 copy-start.1
  84.1 9.5 %collective-permute-start.3 = (bf16[768,128]{1,0:T(8,128)(2,1)S(1)}, bf16[768,128]{1,0:T(8,128)(2,1)S(1)}, u32[]{:S(2)}, u32[]{:S(2)}) collective-permute-start(bf16[768,128]{1,0:T(8,128)(2,1)S(1)} %get-tuple-element.10), channel_id=1, source_target_pairs={{0,1},{1,2},{2,3},{3,0},{4,5},{5,6},{6,7},{7,4},{8,9},{9,10},{10,1... | collective-permute-start | bytes 589832 | tf_op jit(solution)/shard_map/ppermute | solution.py:123
  84.2 12.6 %collective-permute-start.4 = (bf16[768,128]{1,0:T(8,128)(2,1)S(1)}, bf16[768,128]{1,0:T(8,128)(2,1)S(1)}, u32[]{:S(2)}, u32[]{:S(2)}) collective-permute-start(bf16[768,128]{1,0:T(8,128)(2,1)S(1)} %get-tuple-element.12), channel_id=1, source_target_pairs={{0,2},{1,3},{2,0},{3,1},{4,6},{5,7},{6,4},{7,5},{8,10},{9,11},{10,... | collective-permute-start | bytes 589832 | tf_op jit(solution)/shard_map/ppermute | solution.py:123
  87.4 4.5 %copy-start.2 = (bf16[2048,512]{1,0:T(8,128)(2,1)S(1)}, bf16[2048,512]{1,0:T(8,128)(2,1)}, u32[]{:S(2)}) copy-start(bf16[2048,512]{1,0:T(8,128)(2,1)} %copy-done.1) | copy-start | bytes 6291460
  87.4 4.5 %copy-start.4 = (bf16[256,512]{1,0:T(8,128)(2,1)S(1)}, bf16[256,512]{1,0:T(8,128)(2,1)}, u32[]{:S(2)}) copy-start(bf16[256,512]{1,0:T(8,128)(2,1)} %convolution_convert_fusion.3.image_back_ref) | copy-start | bytes 786436
  87.4 9.4 %collective-permute-start.5 = (bf16[768,128]{1,0:T(8,128)(2,1)S(1)}, bf16[768,128]{1,0:T(8,128)(2,1)S(1)}, u32[]{:S(2)}, u32[]{:S(2)}) collective-permute-start(bf16[768,128]{1,0:T(8,128)(2,1)S(1)} %get-tuple-element.11), channel_id=1, source_target_pairs={{0,3},{1,0},{2,1},{3,2},{4,7},{5,4},{6,5},{7,6},{8,11},{9,8},{10,9... | collective-permute-start | bytes 589832 | tf_op jit(solution)/shard_map/ppermute | solution.py:123
  93.6 16.6 %copy-start.7 = (f32[128]{0:T(128)S(1)}, f32[128]{0:T(128)}, u32[]{:S(2)}) copy-start(f32[128]{0:T(128)} %param.11) | copy-start | bytes 1540
  98.9 11.3 %all-to-all-start.2 = ((bf16[8,64,128]{2,1,0:T(8,128)(2,1)}), bf16[8,64,128]{2,1,0:T(8,128)(2,1)S(1)}, u32[]{:S(2)}, u32[]{:S(2)}) async-start(bf16[8,64,128]{2,1,0:T(8,128)(2,1)} %bitcast.13), calls=%async_computation.2 | async-start | bytes 262144 | tf_op jit(solution)/shard_map/all_to_all | solution.py:220
  105.5 28.6 %collective-permute-start.6 = (f32[1024,128]{1,0:T(8,128)S(1)}, f32[1024,128]{1,0:T(8,128)S(1)}, u32[]{:S(2)}, u32[]{:S(2)}) collective-permute-start(f32[1024,128]{1,0:T(8,128)S(1)} %broadcast_multiply_fusion), channel_id=1, source_target_pairs={{0,0},{8,1},{16,2},{24,3},{4,4},{12,5},{20,6},{28,7},{1,8},{9,9},{... | collective-permute-start | bytes 1572872 | tf_op jit(solution)/shard_map/ppermute | solution.py:211
